TPU v7x, 32 devices: a whole 2x2x4 slice. The times are simulated.
32 devices in a mesh: dp: 8 (over z, y), pipe: 4 (over x, core).
Axes of the slice: x: 2, y: 2, z: 4, core: 2. Of those that a mesh axis runs over, the one named last changes fastest.
Arguments:
- inputs: bfloat16 [16, 64, 1024], P(None, 'dp'), may hold values from -6 to 6
- input_weight: bfloat16 [4, 1024, 4096], P('pipe'), may hold values from -0.1875 to 0.1875
- recurrent_weight: bfloat16 [4, 1024, 4096], P('pipe'), may hold values from -0.1875 to 0.1875
- gate_bias: float32 [4, 4096], P('pipe'), may hold values from -4 to 4
- lengths: int32 [64], P('dp'), may hold values from 1 to 16
- cotangent: bfloat16 [4, 16, 64, 1024], P('pipe', None, 'dp'), may hold values from -6 to 6
Outputs:
- grad_input: float32 [4, 1024, 4096], P('pipe', 'dp')
- grad_recurrent: float32 [4, 1024, 4096], P('pipe', 'dp')
- grad_bias: float32 [4, 4096], P('pipe', 'dp')
- final_hidden: bfloat16 [4, 64, 1024], P('pipe', 'dp')
- final_cell: float32 [4, 64, 1024], P('pipe', 'dp')
All inputs are finite; a program needn't handle non-finite values.
Results may differ from a plain program's by a relative error of at most 0.004.
Values may be sent and summed in bfloat16 or wider, within the bound.
A program may use at most 128 MiB of HBM per device.

v0:
```python
from functools import partial

import jax
import jax.numpy as jnp
from jax import lax
from jax.sharding import PartitionSpec as P

BLOCK = 8


def passed_along(block, axis, distance):
    devices = range(lax.axis_size(axis))
    route = [(i - distance, i) for i in devices if i - distance in devices]
    return lax.ppermute(block, axis, route)


def squash(value):
    return 1.0 / (1.0 + jnp.exp(-value))


def activate(pre_act, hidden_width):
    return jnp.concatenate(
        [
            squash(pre_act[:, : 2 * hidden_width]),
            jnp.tanh(pre_act[:, 2 * hidden_width : 3 * hidden_width]),
            squash(pre_act[:, 3 * hidden_width :]),
        ],
        axis=1,
    )


def forward_step(recurrent_weight, gate_bias, carry_state, step_inputs):
    hidden, cell_state = carry_state
    projected, alive_mask = step_inputs
    hidden_width = hidden.shape[1]
    pre_act = (
        projected
        + jnp.dot(hidden, recurrent_weight, preferred_element_type=jnp.float32)
        + gate_bias
    )
    gate_values = activate(pre_act, hidden_width)
    input_gate = gate_values[:, :hidden_width]
    forget_gate = gate_values[:, hidden_width : 2 * hidden_width]
    cell_gate = gate_values[:, 2 * hidden_width : 3 * hidden_width]
    output_gate = gate_values[:, 3 * hidden_width :]
    new_cell = forget_gate * cell_state + input_gate * cell_gate
    cand_hidden = (output_gate * jnp.tanh(new_cell)).astype(jnp.bfloat16)
    kept_cell = alive_mask * new_cell + (1.0 - alive_mask) * cell_state
    kept_hidden = jnp.where(alive_mask > 0, cand_hidden, hidden)
    emitted = jnp.where(alive_mask > 0, cand_hidden, jnp.zeros_like(cand_hidden))
    return ((kept_hidden, kept_cell), (emitted, gate_values, kept_cell, hidden, cell_state))


def backward_step(recurrent_weight, carry_state, step_inputs):
    hidden_grad, cell_grad = carry_state
    upper_grad, own_grad, gate_values, cell_now, cell_prev, alive_mask = step_inputs
    hidden_width = hidden_grad.shape[1]
    input_gate = gate_values[:, :hidden_width]
    forget_gate = gate_values[:, hidden_width : 2 * hidden_width]
    cell_gate = gate_values[:, 2 * hidden_width : 3 * hidden_width]
    output_gate = gate_values[:, 3 * hidden_width :]
    out_grad = alive_mask * (
        hidden_grad + upper_grad.astype(jnp.float32) + own_grad.astype(jnp.float32)
    )
    cell_tanh = jnp.tanh(cell_now)
    through_cell = alive_mask * cell_grad + out_grad * output_gate * (1.0 - cell_tanh * cell_tanh)
    pre_grad = jnp.concatenate(
        [
            through_cell * cell_gate * input_gate * (1.0 - input_gate),
            through_cell * cell_prev * forget_gate * (1.0 - forget_gate),
            through_cell * input_gate * (1.0 - cell_gate * cell_gate),
            out_grad * cell_tanh * output_gate * (1.0 - output_gate),
        ],
        axis=1,
    ).astype(jnp.bfloat16)
    back_hidden = (1.0 - alive_mask) * hidden_grad + lax.dot_general(
        pre_grad, recurrent_weight, (((1,), (1,)), ((), ())), preferred_element_type=jnp.float32
    )
    back_cell = (1.0 - alive_mask) * cell_grad + through_cell * forget_gate
    return ((back_hidden, back_cell), pre_grad)


def contract_rows(left, right):
    return lax.dot_general(
        left, right, (((0,), (0,)), ((), ())), preferred_element_type=jnp.float32
    )


def local(inputs, input_weight, recurrent_weight, gate_bias, lengths, cotangent):
    input_weight = input_weight[0]
    recurrent_weight = recurrent_weight[0]
    gate_bias = gate_bias[0]
    cotangent = cotangent[0]
    frame_total, utterances, hidden_width = inputs.shape
    gate_width = 4 * hidden_width
    section_total = lax.axis_size("pipe")
    section_index = lax.axis_index("pipe")
    frame_span = BLOCK
    block_total = frame_total // frame_span
    tick_total = block_total + section_total - 1
    spare_start = block_total * frame_span
    padded_total = frame_total + frame_span
    alive_all = (jnp.arange(frame_total, dtype=jnp.int32)[:, None] < lengths[None, :]).astype(
        jnp.float32
    )[:, :, None]
    first_section = section_index == 0
    last_section = section_index == section_total - 1

    def run_forward(operands):
        hidden, cell_state, block_in, alive_mask = operands
        projected = jnp.dot(
            block_in.reshape(-1, hidden_width), input_weight, preferred_element_type=jnp.float32
        ).reshape(frame_span, utterances, gate_width)
        new_state, records = lax.scan(
            partial(forward_step, recurrent_weight, gate_bias),
            (hidden, cell_state),
            (projected, alive_mask),
        )
        emitted, gate_values, kept_cells, hidden_prev, cell_prev = records
        return (
            new_state[0],
            new_state[1],
            emitted,
            (gate_values, kept_cells, hidden_prev, cell_prev),
        )

    def skip_forward(operands):
        hidden, cell_state, block_in, alive_mask = operands
        empty_records = (
            jnp.zeros((frame_span, utterances, gate_width), jnp.float32),
            jnp.zeros((frame_span, utterances, hidden_width), jnp.float32),
            jnp.zeros((frame_span, utterances, hidden_width), jnp.bfloat16),
            jnp.zeros((frame_span, utterances, hidden_width), jnp.float32),
        )
        return (hidden, cell_state, jnp.zeros_like(block_in), empty_records)

    hidden = jnp.zeros((utterances, hidden_width), jnp.bfloat16)
    cell_state = jnp.zeros((utterances, hidden_width), jnp.float32)
    stored = (
        jnp.zeros((padded_total, utterances, hidden_width), jnp.bfloat16),
        jnp.zeros((padded_total, utterances, gate_width), jnp.float32),
        jnp.zeros((padded_total, utterances, hidden_width), jnp.float32),
        jnp.zeros((padded_total, utterances, hidden_width), jnp.bfloat16),
        jnp.zeros((padded_total, utterances, hidden_width), jnp.float32),
    )
    emitted = jnp.zeros((frame_span, utterances, hidden_width), jnp.bfloat16)
    for tick_number in range(tick_total):
        if tick_number > 0:
            arrived = passed_along(emitted, "pipe", 1)
        else:
            arrived = emitted
        block_index = tick_number - section_index
        is_active = (block_index >= 0) & (block_index < block_total)
        frame_start = jnp.clip(block_index, 0, block_total - 1) * frame_span
        write_start = jnp.where(is_active, frame_start, spare_start)
        own_block = lax.dynamic_slice_in_dim(inputs, frame_start, frame_span, 0)
        block_in = jnp.where(first_section, own_block, arrived)
        alive_mask = lax.dynamic_slice_in_dim(alive_all, frame_start, frame_span, 0)
        hidden, cell_state, emitted, fresh = lax.cond(
            is_active, run_forward, skip_forward, (hidden, cell_state, block_in, alive_mask)
        )
        fresh = (block_in,) + fresh
        stored = tuple(
            (
                lax.dynamic_update_slice_in_dim(whole, piece, write_start, 0)
                for whole, piece in zip(stored, fresh)
            )
        )
    layer_inputs, gate_all, cell_all, hidden_prev_all, cell_prev_all = stored

    def run_backward(operands):
        hidden_grad, cell_grad, upper_grad, own_grad, frame_start, sums = operands
        alive_mask = lax.dynamic_slice_in_dim(alive_all, frame_start, frame_span, 0)
        gate_values = lax.dynamic_slice_in_dim(gate_all, frame_start, frame_span, 0)
        kept_cells = lax.dynamic_slice_in_dim(cell_all, frame_start, frame_span, 0)
        cell_prev = lax.dynamic_slice_in_dim(cell_prev_all, frame_start, frame_span, 0)
        new_carry, pre_grad = lax.scan(
            partial(backward_step, recurrent_weight),
            (hidden_grad, cell_grad),
            (upper_grad, own_grad, gate_values, kept_cells, cell_prev, alive_mask),
            reverse=True,
        )
        flat_grad = pre_grad.reshape(-1, gate_width)
        lower_grad = (
            lax.dot_general(
                flat_grad,
                input_weight,
                (((1,), (1,)), ((), ())),
                preferred_element_type=jnp.float32,
            )
            .astype(jnp.bfloat16)
            .reshape(frame_span, utterances, hidden_width)
        )
        sums = pre_grad
        return (new_carry[0], new_carry[1], lower_grad, sums)

    def skip_backward(operands):
        hidden_grad, cell_grad, upper_grad, own_grad, frame_start, sums = operands
        sums = jnp.zeros((frame_span, utterances, gate_width), jnp.bfloat16)
        return (hidden_grad, cell_grad, jnp.zeros_like(upper_grad), sums)

    grad_rows = jnp.zeros((padded_total, utterances, gate_width), jnp.bfloat16)
    sums = jnp.zeros((frame_span, utterances, gate_width), jnp.bfloat16)
    hidden_grad = jnp.zeros((utterances, hidden_width), jnp.float32)
    cell_grad = jnp.zeros((utterances, hidden_width), jnp.float32)
    lower_grad = jnp.zeros((frame_span, utterances, hidden_width), jnp.bfloat16)
    for tick_number in range(tick_total):
        if tick_number > 0:
            arrived = passed_along(lower_grad, "pipe", -1)
        else:
            arrived = lower_grad
        offset = tick_number - (section_total - 1 - section_index)
        block_index = block_total - 1 - offset
        is_active = (offset >= 0) & (block_index >= 0)
        frame_start = jnp.clip(block_index, 0, block_total - 1) * frame_span
        own_grad = lax.dynamic_slice_in_dim(cotangent, frame_start, frame_span, 0)
        upper_grad = jnp.where(last_section, jnp.zeros_like(arrived), arrived)
        hidden_grad, cell_grad, lower_grad, sums = lax.cond(
            is_active,
            run_backward,
            skip_backward,
            (hidden_grad, cell_grad, upper_grad, own_grad, frame_start, sums),
        )
        write_start = jnp.where(is_active, frame_start, spare_start)
        grad_rows = lax.dynamic_update_slice_in_dim(grad_rows, sums, write_start, 0)
    flat_grad = grad_rows[:frame_total].reshape(-1, gate_width)
    input_term = contract_rows(layer_inputs[:frame_total].reshape(-1, hidden_width), flat_grad)
    recurrent_term = contract_rows(
        hidden_prev_all[:frame_total].reshape(-1, hidden_width), flat_grad
    )
    bias_term = jnp.sum(flat_grad.astype(jnp.float32), axis=0)
    input_grad, recurrent_grad, bias_grad = (
        lax.psum_scatter(input_term, "dp", scatter_dimension=0, tiled=True),
        lax.psum_scatter(recurrent_term, "dp", scatter_dimension=0, tiled=True),
        lax.psum_scatter(bias_term, "dp", scatter_dimension=0, tiled=True),
    )
    return (input_grad[None], recurrent_grad[None], bias_grad[None], hidden[None], cell_state[None])


def solution(mesh):
    return jax.shard_map(
        local,
        mesh=mesh,
        in_specs=(
            P(None, "dp", None),
            P("pipe", None, None),
            P("pipe", None, None),
            P("pipe", None),
            P("dp"),
            P("pipe", None, "dp", None),
        ),
        out_specs=(
            P("pipe", "dp", None),
            P("pipe", "dp", None),
            P("pipe", "dp"),
            P("pipe", "dp", None),
            P("pipe", "dp", None),
        ),
        check_vma=False,
    )
```

profile of v0, /device:TPU:24, one launch (start us, length us, event | category | flops | bytes accessed | tf_op | source)
XLA Modules:
  0.0 1537.2 jit_solution(7656429736939164740)
XLA Ops:
  11.4 80.8 %conditional.10 = (bf16[8,1024]{1,0:T(8,128)(2,1)}, f32[8,1024]{1,0:T(8,128)}, bf16[8,8,1024]{2,1,0:T(8,128)(2,1)}, f32[8,8,4096]{2,1,0:T(8,128)}, f32[8,8,1024]...) conditional(s32[]{:T(128)} %convert_element_type.297, () %tuple.235, ...), branch_computations={%region_0.1_spmd, %region_1.4_spmd} | conditional | flops 604356608 | bytes 19613262 | solution.py:159
  12.1 4.9 fusion.147
  17.1 75.0 %while.260 = (s32[]{:T(128)}, bf16[8,1024]{1,0:T(8,128)(2,1)}, f32[8,1024]{1,0:T(8,128)}, bf16[8,8,1024]{2,1,0:T(8,128)(2,1)}, f32[8,8,4096]{2,1,0:T(8,128)}, /*...) while((s32[]{:T(128)}, bf16[8,1024]{1,0:T(8,128)(2,1)}, ...), condition=%wide.region_3.3_spmd.clone, body=%wide.region_2.2_spmd.clone.sunk | while | flops 67485712 | bytes 9716606 | solution.py:114
  17.1 4.6 fusion.276
  24.5 4.6 fusion.276
  34.2 4.6 fusion.276
  43.8 4.6 fusion.276
  53.5 4.6 fusion.276
  63.1 4.6 fusion.276
  72.8 4.6 fusion.276
  82.4 4.6 fusion.276
  105.8 90.2 %conditional.11 = (bf16[8,1024]{1,0:T(8,128)(2,1)}, f32[8,1024]{1,0:T(8,128)}, bf16[8,8,1024]{2,1,0:T(8,128)(2,1)}, f32[8,8,4096]{2,1,0:T(8,128)}, f32[8,8,1024]...) conditional(s32[]{:T(128)} %convert_element_type.299, (bf16[8,1024]{1,0:T(8,128)(2,1)}, ...), branch_computations={%region_4.5_spmd, %region_5.8_spmd} | conditional | flops 604315648 | bytes 19547164 | solution.py:159
  107.1 5.9 fusion.10
  113.0 82.0 %while.252 = (s32[]{:T(128)}, bf16[8,1024]{1,0:T(8,128)(2,1)}, f32[8,1024]{1,0:T(8,128)}, bf16[8,8,1024]{2,1,0:T(8,128)(2,1)}, f32[8,8,4096]{2,1,0:T(8,128)}, /*...) while((s32[]{:T(128)}, bf16[8,1024]{1,0:T(8,128)(2,1)}, ...), condition=%wide.region_7.7_spmd, body=%wide.region_6.6_spmd.sunk | while | flops 67444752 | bytes 9716081 | solution.py:114
  113.6 4.6 fusion.272
  123.9 4.6 fusion.272
  134.1 4.6 fusion.272
  144.4 4.6 fusion.272
  175.2 4.6 fusion.272
  208.0 86.6 %collective-permute-start.2 = (bf16[8,8,1024]{2,0,1:T(8,128)(2,1)S(1)}, bf16[8,8,1024]{2,0,1:T(8,128)(2,1)S(1)}, u32[]{:S(2)}, u32[]{:S(2)}) collective-permute-start(bf16[8,8,1024]{2,0,1:T(8,128)(2,1)S(1)} %copy.59), channel_id=1, source_target_pairs={{0,1},{1,2},{2,3},{4,5},{5,6},{6,7},{8,9},{9,10},{10,11},{12,13},{... | collective-permute-start | bytes 393224 | tf_op jit(solution)/shard_map/ppermute | solution.py:14
  326.6 79.3 %collective-permute-done.4 = bf16[8,8,1024]{2,1,0:T(8,128)(2,1)} collective-permute-done((bf16[8,8,1024]{2,1,0:T(8,128)(2,1)}, bf16[8,8,1024]{2,1,0:T(8,128)(2,1)}, u32[]{:S(2)}, u32[]{:S(2)}) %collective-permute-start.4) | collective-permute-done | bytes 131104 | tf_op jit(solution)/shard_map/ppermute | solution.py:14
  416.3 355.1 %collective-permute-done.6 = bf16[8,8,1024]{2,1,0:T(8,128)(2,1)} collective-permute-done((bf16[8,8,1024]{2,1,0:T(8,128)(2,1)}, bf16[8,8,1024]{2,1,0:T(8,128)(2,1)}, u32[]{:S(2)}, u32[]{:S(2)}) %collective-permute-start.6) | collective-permute-done | bytes 131104 | tf_op jit(solution)/shard_map/ppermute | solution.py:14
  771.4 94.7 %conditional.18 = (f32[8,1024]{1,0:T(8,128)}, f32[8,1024]{1,0:T(8,128)}, bf16[8,8,1024]{2,1,0:T(8,128)(2,1)}, bf16[8,8,4096]{2,0,1:T(8,128)(2,1)S(1)}) conditional(s32[]{:T(128)} %convert_element_type.307, (f32[8,1024]{1,0:T(8,128)}, f32[8,1024]{1,0:T(8,128)}) %tuple.251, (pred[8,8,1024]{2,1,0:T(8,128)(4,1)S(1)}, ...), branch_computations={%region_32.33_spmd, %region_33.36_spmd} | conditional | flops 604930048 | bytes 25986134 | solution.py:218
  778.0 80.9 %while.258 = (s32[]{:T(128)}, f32[8,1024]{1,0:T(8,128)}, f32[8,1024]{1,0:T(8,128)}, bf16[8,8,4096]{2,1,0:T(8,128)(2,1)}, f32[8,8,1]{1,2,0:T(1,128)S(1)}, /*index...) while((s32[]{:T(128)}, f32[8,1024]{1,0:T(8,128)}, ...), condition=%wide.region_35.35_spmd, body=%wide.region_34.34_spmd.sunk | while | flops 67928072 | bytes 9404765 | solution.py:177
  781.2 6.3 convolution_add_fusion.16
  791.3 6.3 convolution_add_fusion.16
  801.4 6.3 convolution_add_fusion.16
  811.5 6.3 convolution_add_fusion.16
  821.7 6.3 convolution_add_fusion.16
  831.8 6.3 convolution_add_fusion.16
  841.9 6.3 convolution_add_fusion.16
  852.0 6.3 convolution_add_fusion.16
  858.9 6.9 fusion.114
  872.7 82.6 %conditional.19 = (bf16[8,8,4096]{2,0,1:T(8,128)(2,1)}) conditional(s32[]{:T(128)} %convert_element_type.308, () %tuple.253, (pred[8,8,1024]{2,1,0:T(8,128)(4,1)S(1)}, bf16[8,8,1024]{2,0,1:T(8,128)(2,1)S(1)}, bf16[8,8,1024]{2,1,0:T(8,128)(2,1)}, s32[]{:T(128)}, bf16[1,16,8,1024]{3,2,1,0:T(8,128)(2,1)}, /*index=5*/f32[24,8,4096]{2,1,0:T(8,128)S(1)}, ...), branch_computations={%region_36.37_spmd, %region_37.40_spmd} | conditional | flops 67993616 | bytes 14844962 | solution.py:218
  878.1 76.1 %while.259 = (s32[]{:T(128)}, f32[8,1024]{1,0:T(8,128)}, f32[8,1024]{1,0:T(8,128)}, bf16[8,8,4096]{2,1,0:T(8,128)(2,1)S(1)}, f32[8,8,1]{1,2,0:T(1,128)S(1)}, /*i...) while((s32[]{:T(128)}, f32[8,1024]{1,0:T(8,128)}, ...), condition=%wide.region_39.39_spmd, body=%wide.region_38.38_spmd.sunk | while | flops 67928072 | bytes 9404765 | solution.py:177
  881.4 6.3 convolution_add_fusion.15
  890.9 6.3 convolution_add_fusion.15
  900.4 6.3 convolution_add_fusion.15
  909.9 6.3 convolution_add_fusion.15
  919.4 6.3 convolution_add_fusion.15
  928.9 6.3 convolution_add_fusion.15
  938.5 6.3 convolution_add_fusion.15
  948.0 6.3 convolution_add_fusion.15
  957.2 9.5 convolution_bitcast_fusion
  968.2 8.7 convolution_bitcast_fusion.1
  978.9 34.6 %all-reduce = f32[4096]{0:T(1024)S(1)} all-reduce(f32[4096]{0:T(1024)S(1)} %convert_reduce_fusion), channel_id=4, replica_groups=mesh['dp'=8,'pipe'=4] {'dp'}, use_global_device_ids=true, to_apply=%region_43.44.clone | all-reduce | flops 4096 | bytes 32768
  1014.2 232.0 %reduce-scatter.5.cloned.1.call-done = f32[128,4096]{1,0:T(8,128)} async-done(((f32[1024,4096]{1,0:T(8,128)}), f32[128,4096]{1,0:T(8,128)}) %reduce-scatter.5.cloned.1.call-update) | async-done | bytes 2097168 | tf_op jit(solution)/shard_map/reduce_scatter | solution.py:234
  1246.2 283.7 %reduce-scatter.3.cloned.1.call-done = f32[128,4096]{1,0:T(8,128)} async-done(((f32[1024,4096]{1,0:T(8,128)}), f32[128,4096]{1,0:T(8,128)}) %reduce-scatter.3.cloned.1.call-update) | async-done | bytes 2097168 | tf_op jit(solution)/shard_map/reduce_scatter | solution.py:233
  (361 shorter events, 265.7 us)
Async XLA Ops:
  7.2 1239.0 %reduce-scatter.5.cloned.1.call-start = ((), (), s32[]{:S(2)}) async-start(), calls=%async_computation.3 | async-start | bytes 18874368 | tf_op jit(solution)/shard_map/reduce_scatter | solution.py:234
  10.6 0.8 copy-start.12
  10.6 85.1 %copy-start.15 = (s32[8]{0:T(128)S(1)}, s32[8]{0:T(128)}, u32[]{:S(2)}) copy-start(s32[8]{0:T(128)} %param.50) | copy-start | bytes 100
  11.4 5.7 copy-start.1
  92.1 13.6 copy-start
  93.8 10.3 collective-permute-start
  97.4 0.9 copy-start.2
  197.0 5.2 collective-permute-start.1
  208.0 91.9 %collective-permute-start.2 = (bf16[8,8,1024]{2,0,1:T(8,128)(2,1)S(1)}, bf16[8,8,1024]{2,0,1:T(8,128)(2,1)S(1)}, u32[]{:S(2)}, u32[]{:S(2)}) collective-permute-start(bf16[8,8,1024]{2,0,1:T(8,128)(2,1)S(1)} %copy.59), channel_id=1, source_target_pairs={{0,1},{1,2},{2,3},{4,5},{5,6},{6,7},{8,9},{9,10},{10,11},{12,13},{... | collective-permute-start | bytes 393224 | tf_op jit(solution)/shard_map/ppermute | solution.py:14
  305.0 7.3 collective-permute-start.3
  313.1 7.2 copy-start.10
  313.1 7.2 copy-start.14
  315.6 3.4 copy-start.11
  322.3 1.3 copy-start.9
  322.3 83.6 %collective-permute-start.4 = (bf16[8,8,1024]{2,1,0:T(8,128)(2,1)}, bf16[8,8,1024]{2,1,0:T(8,128)(2,1)}, u32[]{:S(2)}, u32[]{:S(2)}) collective-permute-start(bf16[8,8,1024]{2,1,0:T(8,128)(2,1)} %get-tuple-element.2169), channel_id=1, source_target_pairs={{1,0},{2,1},{3,2},{5,4},{6,5},{7,6},{9,8},{10,9},{11,10},{13,12},{... | collective-permute-start | bytes 393224 | tf_op jit(solution)/shard_map/ppermute | solution.py:14
  324.9 81.0 %copy-start.7 = (bf16[24,8,4096]{2,0,1:T(8,128)(2,1)}, bf16[24,8,4096]{2,0,1:T(8,128)(2,1)S(1)}, u32[]{:S(2)}) copy-start(bf16[24,8,4096]{2,0,1:T(8,128)(2,1)S(1)} %constant_dynamic-update-slice_fusion.9) | copy-start | bytes 4718596
  406.9 6.6 collective-permute-start.5
  414.2 357.2 %collective-permute-start.6 = (bf16[8,8,1024]{2,1,0:T(8,128)(2,1)}, bf16[8,8,1024]{2,1,0:T(8,128)(2,1)}, u32[]{:S(2)}, u32[]{:S(2)}) collective-permute-start(bf16[8,8,1024]{2,1,0:T(8,128)(2,1)} %get-tuple-element.2177), channel_id=1, source_target_pairs={{1,0},{2,1},{3,2},{5,4},{6,5},{7,6},{9,8},{10,9},{11,10},{13,12},{... | collective-permute-start | bytes 393224 | tf_op jit(solution)/shard_map/ppermute | solution.py:14
  858.9 6.9 copy-start.6
  866.1 6.6 collective-permute-start.7
  966.7 1.4 copy-start.8
  966.7 1.5 copy-start.13
  966.7 563.2 %reduce-scatter.3.cloned.1.call-start = ((), (), s32[]{:S(2)}) async-start(), calls=%async_computation.2 | async-start | bytes 18874368 | tf_op jit(solution)/shard_map/reduce_scatter | solution.py:233
  976.8 0.7 copy-start.16
Sparse Core Ops, SparseCore 0:
  966.9 279.2 reduce-scatter.4
  1250.5 279.3 reduce-scatter.2
where the time goes:
time: 1560 us; the launch traced here: 1540 us
  waiting for transfers between devices  959 us (61%)
  matrix products  210 us (13%)
  other arithmetic  134 us (9%)
  starting transfers between devices  97 us (6%)
  local copies, waits for them, and re-layouts  85.9 us (6%)
  blocking collectives  34.6 us (2%)
    ppermute x8, waiting for transfers between devices, passed_along(): return lax.ppermute(block, axis, route)  443 us
    reduce_scatter x1, waiting for transfers between devices, local(): lax.psum_scatter(input_term, 'dp', scatter_dimension=0, tiled=True)  284 us
    reduce_scatter x1, waiting for transfers between devices, local(): lax.psum_scatter(recurrent_term, 'dp', scatter_dimension=0, tiled=True)  232 us
    dot_general x16, matrix products, backward_step(): lax.dot_general(pre_grad, recurrent_weight, (((1,), (1,)), ((), ())), pre...  100 us
    ppermute x8, starting transfers between devices, passed_along(): return lax.ppermute(block, axis, route)  96.9 us
    dot_general x16, matrix products, forward_step(): jnp.dot(hidden, recurrent_weight, preferred_element_type=jnp.float32)  73.3 us
    dynamic_update_slice x48, other arithmetic, run_forward(): lax.scan(partial(forward_step, recurrent_weight, gate_bias), (hidden, cel...  55.7 us
    unnamed x1, blocking collectives  34.6 us
  transfers between devices with their start and end apart: 10, of which 6 were waited for; matrix products, arithmetic and copies ran while one was open for 2% of the time, Pallas kernels for 0%

commit v1 on v0

v1 whole, which is shorter than its diff:
```python
from functools import partial

import jax
import jax.numpy as jnp
from jax import lax
from jax.experimental import pallas as pl
from jax.experimental.pallas import tpu as pltpu
from jax.sharding import PartitionSpec as P

SPAN = 2
MESH = pl.DeviceIdType.MESH
F32 = jnp.float32
BF16 = jnp.bfloat16


def squash(value):
    return 1.0 / (1.0 + jnp.exp(-value))


def rows_of(ref, start):
    pieces = [ref[start + b].astype(F32) for b in range(SPAN)]
    return jnp.concatenate(pieces, axis=0).astype(BF16)


def kernel(
    dp_total, pipe_total, own_width, share,
    inputs, input_weight, recurrent_weight, bias, alive, cotangent,
    dpre_all, x_all, h_all, final_hidden, final_cell,
    w, r, xin, y, hist, cells, gates, proj, dpre, upper, lower, dh, dc,
    load_sem, fsend, frecv, bsend, brecv, dsend, drecv, xsend, xrecv, hsend, hrecv, local_sem,
):
    frames, utterances, width = xin.shape
    blocks = frames // SPAN
    me = lax.axis_index("dp")
    stage = lax.axis_index("pipe")
    first = stage == 0
    last = stage == pipe_total - 1

    load_w = pltpu.make_async_copy(input_weight, w, load_sem.at[0])
    load_r = pltpu.make_async_copy(recurrent_weight, r, load_sem.at[1])
    load_x = pltpu.make_async_copy(inputs, xin, load_sem.at[2])

    @pl.when(first)
    def _():
        load_x.start()

    load_w.start()
    load_r.start()

    barrier = pltpu.get_barrier_semaphore()

    def greet(j, carry):
        peer = lax.rem(me + j, dp_total)
        pl.semaphore_signal(barrier, inc=1, device_id=(peer, stage), device_id_type=MESH)
        return carry

    lax.fori_loop(1, dp_total, greet, 0)

    for near in (1, pipe_total - 1):
        neighbour = lax.rem(stage + near, pipe_total)
        pl.semaphore_signal(barrier, inc=1, device_id=(me, neighbour), device_id_type=MESH)
    pl.semaphore_wait(barrier, dp_total + 1)

    def up(k):
        part = pl.ds(k * SPAN, SPAN)
        return pltpu.make_async_remote_copy(
            src_ref=y.at[part], dst_ref=xin.at[part], send_sem=fsend.at[k], recv_sem=frecv.at[k],
            device_id=(me, lax.rem(stage + 1, pipe_total)), device_id_type=MESH,
        )

    def down(k):
        part = pl.ds(k * SPAN, SPAN)
        return pltpu.make_async_remote_copy(
            src_ref=lower.at[part], dst_ref=upper.at[part], send_sem=bsend.at[k], recv_sem=brecv.at[k],
            device_id=(me, lax.rem(stage + pipe_total - 1, pipe_total)), device_id_type=MESH,
        )

    def spread(j, part, slot):
        peer = lax.rem(me + j, dp_total)
        return pltpu.make_async_remote_copy(
            src_ref=dpre.at[part], dst_ref=dpre_all.at[slot, part],
            send_sem=dsend.at[j - 1], recv_sem=drecv.at[j - 1],
            device_id=(peer, stage), device_id_type=MESH,
        )

    def columns(peer):
        return pl.ds(pl.multiple_of(((peer * own_width) // share) * share, 128), share)

    def hand_x(j, slot):
        peer = lax.rem(me + j, dp_total)
        return pltpu.make_async_remote_copy(
            src_ref=xin.at[:, :, columns(peer)], dst_ref=x_all.at[slot],
            send_sem=xsend.at[j - 1], recv_sem=xrecv.at[j - 1],
            device_id=(peer, stage), device_id_type=MESH,
        )

    def hand_h(j, slot):
        peer = lax.rem(me + j, dp_total)
        return pltpu.make_async_remote_copy(
            src_ref=hist.at[pl.ds(0, frames), :, columns(peer)], dst_ref=h_all.at[slot],
            send_sem=hsend.at[j - 1], recv_sem=hrecv.at[j - 1],
            device_id=(peer, stage), device_id_type=MESH,
        )

    own_x = pltpu.make_async_copy(xin.at[:, :, columns(me)], x_all.at[me], local_sem.at[0])
    own_h = pltpu.make_async_copy(
        hist.at[pl.ds(0, frames), :, columns(me)], h_all.at[me], local_sem.at[1]
    )
    own_d = pltpu.make_async_copy(dpre, dpre_all.at[me], local_sem.at[2])

    hist[0] = jnp.zeros((utterances, width), BF16)
    cells[0] = jnp.zeros((utterances, width), F32)

    @pl.when(first)
    def _():
        load_x.wait()

    load_w.wait()
    load_r.wait()

    def forward_block(k, carry):
        start = k * SPAN

        @pl.when(stage > 0)
        def _():
            up(k).wait_recv()

        got = jnp.dot(rows_of(xin, start), w[...], preferred_element_type=F32)
        for b in range(SPAN):
            proj[b] = got[b * utterances : (b + 1) * utterances]

        def step(b, inner):
            t = start + b
            hidden = hist[t]
            cell = cells[t]
            live = alive[t][:, :1]
            pre = proj[b] + jnp.dot(hidden, r[...], preferred_element_type=F32) + bias[...]
            i = squash(pre[:, :width])
            f = squash(pre[:, width : 2 * width])
            g = jnp.tanh(pre[:, 2 * width : 3 * width])
            o = squash(pre[:, 3 * width :])
            gates[t, :, pl.ds(0, width)] = i
            gates[t, :, pl.ds(width, width)] = f
            gates[t, :, pl.ds(2 * width, width)] = g
            gates[t, :, pl.ds(3 * width, width)] = o
            new_cell = f * cell + i * g
            cand = o * jnp.tanh(new_cell)
            cells[t + 1] = live * new_cell + (1.0 - live) * cell
            hist[t + 1] = jnp.where(live > 0, cand, hidden.astype(F32)).astype(BF16)
            y[t] = jnp.where(live > 0, cand, 0.0).astype(BF16)
            return inner

        lax.fori_loop(0, SPAN, step, 0)

        @pl.when(stage < pipe_total - 1)
        def _():
            up(k).start()

        return carry

    lax.fori_loop(0, blocks, forward_block, 0)
    final_hidden[...] = hist[frames]
    final_cell[...] = cells[frames]

    def hand(j, carry):
        hand_x(j, me).start()
        hand_h(j, me).start()
        return carry

    lax.fori_loop(1, dp_total, hand, 0)
    own_x.start()
    own_h.start()

    dh[...] = jnp.zeros(dh.shape, F32)
    dc[...] = jnp.zeros(dc.shape, F32)

    @pl.when(last)
    def _():
        upper[...] = jnp.zeros(upper.shape, BF16)

    nt = (((1,), (1,)), ((), ()))

    def backward_block(n, carry):
        k = blocks - 1 - n
        start = k * SPAN

        @pl.when(stage < pipe_total - 1)
        def _():
            down(k).wait_recv()

        def step(m, inner):
            t = start + SPAN - 1 - m
            live = alive[t][:, :1]
            i = gates[t, :, pl.ds(0, width)]
            f = gates[t, :, pl.ds(width, width)]
            g = gates[t, :, pl.ds(2 * width, width)]
            o = gates[t, :, pl.ds(3 * width, width)]
            e = live * (dh[...] + upper[t].astype(F32) + cotangent[t].astype(F32))
            tanh_c = jnp.tanh(cells[t + 1])
            dcell = live * dc[...] + e * o * (1.0 - tanh_c * tanh_c)
            dpre[t, :, pl.ds(0, width)] = (dcell * g * i * (1.0 - i)).astype(BF16)
            dpre[t, :, pl.ds(width, width)] = (dcell * cells[t] * f * (1.0 - f)).astype(BF16)
            dpre[t, :, pl.ds(2 * width, width)] = (dcell * i * (1.0 - g * g)).astype(BF16)
            dpre[t, :, pl.ds(3 * width, width)] = (e * tanh_c * o * (1.0 - o)).astype(BF16)
            back = lax.dot_general(dpre[t], r[...], nt, preferred_element_type=F32)
            dh[...] = (1.0 - live) * dh[...] + back
            dc[...] = (1.0 - live) * dc[...] + dcell * f
            return inner

        lax.fori_loop(0, SPAN, step, 0)

        @pl.when(stage > 0)
        def _():
            got = lax.dot_general(rows_of(dpre, start), w[...], nt, preferred_element_type=F32)
            for b in range(SPAN):
                lower[start + b] = got[b * utterances : (b + 1) * utterances].astype(BF16)
            down(k).start()

        def send(j, inner):
            spread(j, pl.ds(start, SPAN), me).start()
            return inner

        lax.fori_loop(1, dp_total, send, 0)
        return carry

    lax.fori_loop(0, blocks, backward_block, 0)
    own_d.start()

    def settle(j, carry):
        source = lax.rem(me + dp_total - j, dp_total)
        for copy in (hand_x(j, source), hand_h(j, source), spread(j, pl.ds(0, frames), source)):
            copy.wait_send()
            copy.wait_recv()
        return carry

    lax.fori_loop(1, dp_total, settle, 0)

    def drain(k, carry):
        @pl.when(stage < pipe_total - 1)
        def _():
            up(k).wait_send()

        @pl.when(stage > 0)
        def _():
            down(k).wait_send()

        return carry

    lax.fori_loop(0, blocks, drain, 0)
    own_x.wait()
    own_h.wait()
    own_d.wait()


def contract_rows(left, right):
    return lax.dot_general(
        left, right, (((0,), (0,)), ((), ())), preferred_element_type=F32
    )


def local(inputs, input_weight, recurrent_weight, gate_bias, lengths, cotangent):
    frames, utterances, width = inputs.shape
    gate_width = 4 * width
    dp_total = lax.axis_size("dp")
    pipe_total = lax.axis_size("pipe")
    me = lax.axis_index("dp")
    own_width = width // dp_total
    share = max(own_width, 128)
    blocks = frames // SPAN
    live = (jnp.arange(frames, dtype=jnp.int32)[:, None] < lengths[None, :]).astype(F32)
    live = jnp.broadcast_to(live[:, :, None], (frames, utterances, 128))
    vmem = pl.BlockSpec(memory_space=pltpu.VMEM)
    hbm = pl.BlockSpec(memory_space=pl.ANY)
    dma = pltpu.SemaphoreType.DMA
    dpre_all, x_all, h_all, hidden, cell = pl.pallas_call(
        partial(kernel, dp_total, pipe_total, own_width, share),
        out_shape=(
            jax.ShapeDtypeStruct((dp_total, frames, utterances, gate_width), BF16),
            jax.ShapeDtypeStruct((dp_total, frames, utterances, share), BF16),
            jax.ShapeDtypeStruct((dp_total, frames, utterances, share), BF16),
            jax.ShapeDtypeStruct((utterances, width), BF16),
            jax.ShapeDtypeStruct((utterances, width), F32),
        ),
        in_specs=[hbm, hbm, hbm, vmem, vmem, vmem],
        out_specs=(hbm, hbm, hbm, vmem, vmem),
        scratch_shapes=[
            pltpu.VMEM((width, gate_width), BF16),
            pltpu.VMEM((width, gate_width), BF16),
            pltpu.VMEM((frames, utterances, width), BF16),
            pltpu.VMEM((frames, utterances, width), BF16),
            pltpu.VMEM((frames + 1, utterances, width), BF16),
            pltpu.VMEM((frames + 1, utterances, width), F32),
            pltpu.VMEM((frames, utterances, gate_width), F32),
            pltpu.VMEM((SPAN, utterances, gate_width), F32),
            pltpu.VMEM((frames, utterances, gate_width), BF16),
            pltpu.VMEM((frames, utterances, width), BF16),
            pltpu.VMEM((frames, utterances, width), BF16),
            pltpu.VMEM((utterances, width), F32),
            pltpu.VMEM((utterances, width), F32),
            dma((3,)),
            dma((blocks,)),
            dma((blocks,)),
            dma((blocks,)),
            dma((blocks,)),
            dma((dp_total - 1,)),
            dma((dp_total - 1,)),
            dma((dp_total - 1,)),
            dma((dp_total - 1,)),
            dma((dp_total - 1,)),
            dma((dp_total - 1,)),
            dma((3,)),
        ],
        compiler_params=pltpu.CompilerParams(
            collective_id=0, has_side_effects=True, vmem_limit_bytes=48 * 1024 * 1024
        ),
    )(inputs, input_weight[0], recurrent_weight[0], gate_bias, live, cotangent[0])
    if share > own_width:
        offset = (me * own_width) % share
        x_all = lax.dynamic_slice_in_dim(x_all, offset, own_width, 3)
        h_all = lax.dynamic_slice_in_dim(h_all, offset, own_width, 3)
    rows = dpre_all.reshape(-1, gate_width)
    input_grad = contract_rows(x_all.reshape(-1, own_width), rows)
    recurrent_grad = contract_rows(h_all.reshape(-1, own_width), rows)
    bias_width = gate_width // dp_total
    mine = lax.dynamic_slice_in_dim(rows, me * bias_width, bias_width, 1)
    bias_grad = jnp.sum(mine.astype(F32), axis=0)
    return (input_grad[None], recurrent_grad[None], bias_grad[None], hidden[None], cell[None])


def solution(mesh):
    return jax.shard_map(
        local,
        mesh=mesh,
        in_specs=(
            P(None, "dp", None),
            P("pipe", None, None),
            P("pipe", None, None),
            P("pipe", None),
            P("dp"),
            P("pipe", None, "dp", None),
        ),
        out_specs=(
            P("pipe", "dp", None),
            P("pipe", "dp", None),
            P("pipe", "dp"),
            P("pipe", "dp", None),
            P("pipe", "dp", None),
        ),
        check_vma=False,
    )
```

time: 1560 us -> 275 us (0.18); the launches traced: 1540 us -> 273 us
  waiting for transfers between devices: 959 us -> 0 us
  Pallas kernels: 0 us -> 256 us
  matrix products: 210 us -> 8.8 us
  other arithmetic: 134 us -> 2.67 us
  starting transfers between devices: 97 us -> 0 us
  local copies, waits for them, and re-layouts: 85.9 us -> 3.92 us
  blocking collectives: 34.6 us -> 0 us
    reduce_scatter x2 -> x0, waiting for transfers between devices: 516 us -> none  [the longest x1 284 us: local(): lax.psum_scatter(input_term, 'dp', scatter_dimension=0, tiled=True)]
    ppermute x8 -> x0, waiting for transfers between devices: 443 us -> none  [passed_along(): return lax.ppermute(block, axis, route)]
    pallas_call x0 -> x1, Pallas kernels: none -> 256 us  [local(): pl.pallas_call(partial(kernel, dp_total, pipe_total, own_width, share), o...]
    dot_general x35 -> x0, matrix products: 191 us -> none  [the longest x16 100 us: backward_step(): lax.dot_general(pre_grad, recurrent_weight, (((1,), (1,)), ((), ())), pre...]
    ppermute x8 -> x0, starting transfers between devices: 96.9 us -> none  [passed_along(): return lax.ppermute(block, axis, route)]
    dynamic_update_slice x69 -> x0, other arithmetic: 65.8 us -> none  [the longest x48 55.7 us: run_forward(): lax.scan(partial(forward_step, recurrent_weight, gate_bias), (hidden, cel...]
    unnamed x1 -> x0, blocking collectives: 34.6 us -> none
    dynamic_update_slice x24 -> x0, local copies, waits for them, and re-layouts: 31.1 us -> none  [the longest x19 25.6 us: local(): lax.dynamic_update_slice_in_dim(whole, piece, write_start, 0)]
  transfers between devices with their start and end apart: 10 -> 0, of which waited for: 6 -> 0; matrix products, arithmetic and copies ran while one was open for 2% -> 0% of each run, Pallas kernels for 0% -> 0%
where the time goes in v1:
time: 275 us; the launch traced here: 273 us
  Pallas kernels  256 us (93%)
  matrix products  8.8 us (3%)
  local copies, waits for them, and re-layouts  3.92 us (1%)
    pallas_call x1, Pallas kernels, local(): pl.pallas_call(partial(kernel, dp_total, pipe_total, own_width, share), o...  256 us
    dot_general x2, matrix products, contract_rows(): lax.dot_general(left, right, (((0,), (0,)), ((), ())), preferred_element_...  8.8 us

profile of v1, /device:TPU:24, one launch (start us, length us, event | category | flops | bytes accessed | tf_op | source)
XLA Modules:
  0.0 272.5 jit_solution(345845021927845773)
XLA Ops:
  0.6 0.7 fusion
  1.3 0.1 broadcast_in_dim.23.alive
  1.4 0.0 copy-start
  1.4 1.0 copy-done
  2.3 0.0 copy-start.1
  2.3 0.9 copy-done.1
  3.3 0.0 copy-start.2
  3.3 0.7 copy-done.2
  4.0 256.5 %shard_map.101 = (bf16[8,16,8,4096]{3,2,1,0:T(8,128)(2,1)}, bf16[8,16,8,128]{3,2,1,0:T(8,128)(2,1)S(1)}, bf16[8,16,8,128]{3,2,1,0:T(8,128)(2,1)S(1)}, bf16[8,1024]{1,0:T(8,128)(2,1)S(1)}, f32[8,1024]{1,0:T(8,128)S(1)}) custom-call(bf16[16,8,1024]{2,1,0:T(8,128)(2,1)S(1)} %copy-done, bf16[1024,4096]{1,0:T(8,128)(2,1)} %bitcast.27, ...), custom_call_target="tpu_custom_call" | custom-call | tf_op jit(solution)/shard_map/pallas_call | solution.py:275
  260.5 0.0 copy-start.3
  260.5 6.2 %convolution_bitcast_fusion.1 = f32[1,128,4096]{2,1,0:T(8,128)} fusion(bf16[8,16,8,128]{3,2,1,0:T(8,128)(2,1)S(1)} %get-tuple-element.10, bf16[8,16,8,4096]{3,2,1,0:T(8,128)(2,1)} %get-tuple-element.11), kind=kOutput, calls=%fused_computation.1 | convolution fusion | flops 1073741824 | bytes 10747904 | tf_op jit(solution)/shard_map/dot_general | solution.py:256
  266.6 0.0 copy-done.3
  266.6 2.6 convolution_bitcast_fusion
  269.3 2.0 convert_reduce_fusion
  271.3 0.6 copy.23
  271.9 0.6 copy.24
Async XLA Ops:
  1.4 1.0 copy-start
  2.3 0.9 copy-start.1
  3.3 0.7 copy-start.2
  260.5 6.2 %copy-start.3 = (bf16[8,16,8,4096]{3,2,1,0:T(8,128)(2,1)S(1)}, bf16[8,16,8,4096]{3,2,1,0:T(8,128)(2,1)}, u32[]{:S(2)}) copy-start(bf16[8,16,8,4096]{3,2,1,0:T(8,128)(2,1)} %get-tuple-element.11) | copy-start | bytes 25165828

commit v2 on v1

--- a/solution.py
+++ b/solution.py
@@ -26,8 +26,8 @@
     dp_total, pipe_total, own_width, share,
     inputs, input_weight, recurrent_weight, bias, alive, cotangent,
     dpre_all, x_all, h_all, final_hidden, final_cell,
-    w, r, xin, y, hist, cells, gates, proj, dpre, upper, lower, dh, dc,
-    load_sem, fsend, frecv, bsend, brecv, dsend, drecv, xsend, xrecv, hsend, hrecv, local_sem,
+    w, r, w_turned, r_turned, xin, y, hist, cells, gates, proj, dpre, upper, lower, dh, dc,
+    load_sem, fsend, frecv, bsend, brecv, psend, precv, dsend, drecv, wsend, wrecv, xsend, xrecv, hsend, hrecv, local_sem,
 ):
     frames, utterances, width = xin.shape
     blocks = frames // SPAN
@@ -75,13 +75,53 @@
             device_id=(me, lax.rem(stage + pipe_total - 1, pipe_total)), device_id_type=MESH,
         )
 
-    def spread(j, part, slot):
-        peer = lax.rem(me + j, dp_total)
+    partner = me + 1 - 2 * lax.rem(me, 2)
+
+    def to_partner(part, slot):
         return pltpu.make_async_remote_copy(
             src_ref=dpre.at[part], dst_ref=dpre_all.at[slot, part],
-            send_sem=dsend.at[j - 1], recv_sem=drecv.at[j - 1],
+            send_sem=psend.at[0], recv_sem=precv.at[0],
+            device_id=(partner, stage), device_id_type=MESH,
+        )
+
+    def spread(j, k, part, slot):
+        peer = lax.rem(me + 2 * j, dp_total)
+        return pltpu.make_async_remote_copy(
+            src_ref=dpre.at[part], dst_ref=dpre_all.at[slot, part],
+            send_sem=dsend.at[j - 1], recv_sem=drecv.at[(j - 1) * blocks + k],
             device_id=(peer, stage), device_id_type=MESH,
         )
+
+    def relay(j, part, slot):
+        return pltpu.make_async_remote_copy(
+            src_ref=dpre_all.at[slot, part], dst_ref=dpre_all.at[slot, part],
+            send_sem=wsend.at[j - 1], recv_sem=wrecv.at[j - 1],
+            device_id=(partner, stage), device_id_type=MESH,
+        )
+
+    def source_of(device, j):
+        return lax.rem(device + dp_total - 2 * j, dp_total)
+
+    def relay_block(k):
+        part = pl.ds(k * SPAN, SPAN)
+
+        def one(j, inner):
+            source = source_of(me, j)
+            spread(j, k, part, source).wait_recv()
+            relay(j, part, source).start()
+            return inner
+
+        lax.fori_loop(1, dp_total // 2, one, 0)
+
+    tile = 256
+
+    def turn(c, carry):
+        cut = pl.ds(pl.multiple_of(c * tile, tile), tile)
+        r_turned[cut, :] = r[:, cut].T
+        w_turned[cut, :] = w[:, cut].T
+        return carry
+
+    turns = w.shape[1] // tile
 
     def columns(peer):
         return pl.ds(pl.multiple_of(((peer * own_width) // share) * share, 128), share)
@@ -116,7 +156,12 @@
         load_x.wait()
 
     load_w.wait()
-    load_r.wait()
+
+    @pl.when(stage >= pipe_total // 2)
+    def _():
+        load_r.wait()
+        lax.fori_loop(0, turns, turn, 0)
+
 
     def forward_block(k, carry):
         start = k * SPAN
@@ -128,6 +173,10 @@
         got = jnp.dot(rows_of(xin, start), w[...], preferred_element_type=F32)
         for b in range(SPAN):
             proj[b] = got[b * utterances : (b + 1) * utterances]
+
+        @pl.when((k == 0) & (stage < pipe_total // 2))
+        def _():
+            load_r.wait()
 
         def step(b, inner):
             t = start + b
@@ -171,14 +220,16 @@
     own_x.start()
     own_h.start()
 
+    @pl.when(stage < pipe_total // 2)
+    def _():
+        lax.fori_loop(0, turns, turn, 0)
+
     dh[...] = jnp.zeros(dh.shape, F32)
     dc[...] = jnp.zeros(dc.shape, F32)
 
     @pl.when(last)
     def _():
         upper[...] = jnp.zeros(upper.shape, BF16)
-
-    nt = (((1,), (1,)), ((), ()))
 
     def backward_block(n, carry):
         k = blocks - 1 - n
@@ -202,7 +253,7 @@
             dpre[t, :, pl.ds(width, width)] = (dcell * cells[t] * f * (1.0 - f)).astype(BF16)
             dpre[t, :, pl.ds(2 * width, width)] = (dcell * i * (1.0 - g * g)).astype(BF16)
             dpre[t, :, pl.ds(3 * width, width)] = (e * tanh_c * o * (1.0 - o)).astype(BF16)
-            back = lax.dot_general(dpre[t], r[...], nt, preferred_element_type=F32)
+            back = jnp.dot(dpre[t], r_turned[...], preferred_element_type=F32)
             dh[...] = (1.0 - live) * dh[...] + back
             dc[...] = (1.0 - live) * dc[...] + dcell * f
             return inner
@@ -211,29 +262,47 @@
 
         @pl.when(stage > 0)
         def _():
-            got = lax.dot_general(rows_of(dpre, start), w[...], nt, preferred_element_type=F32)
+            got = jnp.dot(rows_of(dpre, start), w_turned[...], preferred_element_type=F32)
             for b in range(SPAN):
                 lower[start + b] = got[b * utterances : (b + 1) * utterances].astype(BF16)
             down(k).start()
 
         def send(j, inner):
-            spread(j, pl.ds(start, SPAN), me).start()
+            spread(j, k, pl.ds(start, SPAN), me).start()
             return inner
 
-        lax.fori_loop(1, dp_total, send, 0)
+        lax.fori_loop(1, dp_total // 2, send, 0)
+        to_partner(pl.ds(start, SPAN), me).start()
+
+        @pl.when(n > 0)
+        def _():
+            relay_block(k + 1)
+
         return carry
 
     lax.fori_loop(0, blocks, backward_block, 0)
     own_d.start()
+    relay_block(0)
 
     def settle(j, carry):
         source = lax.rem(me + dp_total - j, dp_total)
-        for copy in (hand_x(j, source), hand_h(j, source), spread(j, pl.ds(0, frames), source)):
+        for copy in (hand_x(j, source), hand_h(j, source)):
             copy.wait_send()
             copy.wait_recv()
         return carry
 
     lax.fori_loop(1, dp_total, settle, 0)
+    whole = pl.ds(0, frames)
+
+    def settle_dpre(j, carry):
+        spread(j, 0, whole, me).wait_send()
+        relay(j, whole, source_of(me, j)).wait_send()
+        relay(j, whole, source_of(partner, j)).wait_recv()
+        return carry
+
+    lax.fori_loop(1, dp_total // 2, settle_dpre, 0)
+    to_partner(whole, me).wait_send()
+    to_partner(whole, partner).wait_recv()
 
     def drain(k, carry):
         @pl.when(stage < pipe_total - 1)
@@ -286,6 +355,8 @@
         scratch_shapes=[
             pltpu.VMEM((width, gate_width), BF16),
             pltpu.VMEM((width, gate_width), BF16),
+            pltpu.VMEM((gate_width, width), BF16),
+            pltpu.VMEM((gate_width, width), BF16),
             pltpu.VMEM((frames, utterances, width), BF16),
             pltpu.VMEM((frames, utterances, width), BF16),
             pltpu.VMEM((frames + 1, utterances, width), BF16),
@@ -302,8 +373,12 @@
             dma((blocks,)),
             dma((blocks,)),
             dma((blocks,)),
-            dma((dp_total - 1,)),
-            dma((dp_total - 1,)),
+            dma((1,)),
+            dma((1,)),
+            dma((dp_total // 2 - 1,)),
+            dma(((dp_total // 2 - 1) * blocks,)),
+            dma((dp_total // 2 - 1,)),
+            dma((dp_total // 2 - 1,)),
             dma((dp_total - 1,)),
             dma((dp_total - 1,)),
             dma((dp_total - 1,)),
@@ -311,7 +386,7 @@
             dma((3,)),
         ],
         compiler_params=pltpu.CompilerParams(
-            collective_id=0, has_side_effects=True, vmem_limit_bytes=48 * 1024 * 1024
+            collective_id=0, has_side_effects=True, vmem_limit_bytes=52 * 1024 * 1024
         ),
     )(inputs, input_weight[0], recurrent_weight[0], gate_bias, live, cotangent[0])
     if share > own_width:

time: 275 us -> 193 us (0.70)
  Pallas kernels: 256 us -> 177 us
    pallas_call x1, Pallas kernels: 256 us -> 177 us  [local(): pl.pallas_call(partial(kernel, dp_total, pipe_total, own_width, share), o...]
where the time goes in v2:
time: 193 us
  Pallas kernels  177 us (92%)
  matrix products  8.8 us (5%)
  local copies, waits for them, and re-layouts  3.92 us (2%)
  other arithmetic  2.67 us (1%)
    pallas_call x1, Pallas kernels, local(): pl.pallas_call(partial(kernel, dp_total, pipe_total, own_width, share), o...  177 us
    dot_general x2, matrix products, contract_rows(): lax.dot_general(left, right, (((0,), (0,)), ((), ())), preferred_element_...  8.8 us

profile of v2, /device:TPU:24, one launch (start us, length us, event | category | flops | bytes accessed | tf_op | source)
XLA Modules:
  0.0 193.1 jit_solution(16827078844607012253)
XLA Ops:
  0.6 0.7 fusion
  1.3 0.1 broadcast_in_dim.23.alive
  1.4 0.0 copy-start
  1.4 1.0 copy-done
  2.3 0.0 copy-start.1
  2.3 0.9 copy-done.1
  3.3 0.0 copy-start.2
  3.3 0.7 copy-done.2
  4.0 177.1 %shard_map.101 = (bf16[8,16,8,4096]{3,2,1,0:T(8,128)(2,1)}, bf16[8,16,8,128]{3,2,1,0:T(8,128)(2,1)S(1)}, bf16[8,16,8,128]{3,2,1,0:T(8,128)(2,1)S(1)}, bf16[8,1024]{1,0:T(8,128)(2,1)S(1)}, f32[8,1024]{1,0:T(8,128)S(1)}) custom-call(bf16[16,8,1024]{2,1,0:T(8,128)(2,1)S(1)} %copy-done, bf16[1024,4096]{1,0:T(8,128)(2,1)} %bitcast.27, ...), custom_call_target="tpu_custom_call" | custom-call | tf_op jit(solution)/shard_map/pallas_call | solution.py:344
  181.1 0.0 copy-start.3
  181.1 6.2 %convolution_bitcast_fusion.1 = f32[1,128,4096]{2,1,0:T(8,128)} fusion(bf16[8,16,8,128]{3,2,1,0:T(8,128)(2,1)S(1)} %get-tuple-element.10, bf16[8,16,8,4096]{3,2,1,0:T(8,128)(2,1)} %get-tuple-element.11), kind=kOutput, calls=%fused_computation.1 | convolution fusion | flops 1073741824 | bytes 10747904 | tf_op jit(solution)/shard_map/dot_general | solution.py:325
  187.3 0.0 copy-done.3
  187.3 2.6 %convolution_bitcast_fusion = f32[1,128,4096]{2,1,0:T(8,128)} fusion(bf16[8,16,8,128]{3,2,1,0:T(8,128)(2,1)S(1)} %get-tuple-element.12, bf16[8,16,8,4096]{3,2,1,0:T(8,128)(2,1)S(1)} %copy-done.3), kind=kOutput, calls=%fused_computation | convolution fusion | flops 1073741824 | bytes 10747904 | tf_op jit(solution)/shard_map/dot_general | solution.py:325
  189.9 2.0 %convert_reduce_fusion = f32[512]{0:T(512)} fusion(bf16[1024,4096]{1,0:T(8,128)(2,1)} %bitcast.26, s32[]{:T(128)S(6)} %select_n.3), kind=kLoop, calls=%fused_computation.2 | loop fusion | flops 1048064 | bytes 1050628 | tf_op jit(solution)/shard_map/reduce_sum | solution.py:401
  191.9 0.6 copy.23
  192.5 0.6 copy.24
Async XLA Ops:
  1.4 1.0 copy-start
  2.3 0.9 copy-start.1
  3.3 0.7 copy-start.2
  181.1 6.2 %copy-start.3 = (bf16[8,16,8,4096]{3,2,1,0:T(8,128)(2,1)S(1)}, bf16[8,16,8,4096]{3,2,1,0:T(8,128)(2,1)}, u32[]{:S(2)}) copy-start(bf16[8,16,8,4096]{3,2,1,0:T(8,128)(2,1)} %get-tuple-element.11) | copy-start | bytes 25165828
